TPU v7x, 32 devices: a whole 2x2x4 slice. The times are simulated.
32 devices in a mesh: band: 8 (over z, x), patch: 4 (over y, core).
Axes of the slice: x: 2, y: 2, z: 4, core: 2. Of those that a mesh axis runs over, the one named last changes fastest.
Arguments:
- latents: bfloat16 [8, 10240, 512], P('band', 'patch'), may hold values from -6 to 6
- owners: int32 [16], replicated, may hold values from 0 to 3, as said below
- block_rows: int32 [16, 128], replicated, may hold values from 0 to 2559
- interp_weights: bfloat16 [16, 1024, 128], P('band', 'patch'), may hold values from -0.5 to 0.5
- w_first: bfloat16 [8, 512, 512], P('band'), may hold values from -0.25 to 0.25
- b_first: float32 [8, 512], P('band'), may hold values from -3 to 3
- w_second: bfloat16 [8, 512, 512], P('band'), may hold values from -0.25 to 0.25
- b_second: float32 [8, 512], P('band'), may hold values from -4 to 4
- gain: float32 [8, 512], P('band'), may hold values from 0.1 to 1.9
- w_out: bfloat16 [8, 12, 512], P('band'), may hold values from -0.25 to 0.25
- b_out: float32 [8, 12], P('band'), may hold values from -4 to 4
Outputs:
- grid_fields: float32 [8, 12, 16384], P('band', None, 'patch')
Inputs may be any that keep to these rules, and one draw needn't show every extreme that they name: `owners`: no patch owns more than 8 tiles, and one patch owns exactly 8.
All inputs are finite; a program needn't handle non-finite values.
Results may differ from a plain program's by a relative error of at most 0.003.
Values may be sent and summed in bfloat16 or wider, within the bound.
A program may use at most 64 MiB of HBM per device.

v0:
```python
import jax
import jax.numpy as jnp
from jax import lax
from jax.sharding import PartitionSpec as P


def decode_rows(interp, w_first, b_first, w_second, b_second, gain, w_out, b_out):
    hidden = jax.nn.silu(
        jnp.dot(interp, w_first, preferred_element_type=jnp.float32) + b_first
    ).astype(jnp.bfloat16)
    second = jnp.dot(hidden, w_second, preferred_element_type=jnp.float32) + b_second
    mean_value = jnp.mean(second, axis=-1, keepdims=True)
    centred = second - mean_value
    variance = jnp.mean(centred * centred, axis=-1, keepdims=True)
    normed = (centred * lax.rsqrt(variance + 1e-05) * gain).astype(jnp.bfloat16)
    result = lax.dot_general(
        w_out, normed, (((1,), (1,)), ((), ())), preferred_element_type=jnp.float32
    )
    return result + b_out[:, None]


def body(
    latents,
    owners,
    block_rows,
    interp_weights,
    w_first,
    b_first,
    w_second,
    b_second,
    gain,
    w_out,
    b_out,
):
    tile_count = owners.shape[0]
    cell_count = interp_weights.shape[1]
    channels = w_out.shape[1]
    local_latents = latents[0]
    width = local_latents.shape[1]
    weights_all = lax.all_gather(interp_weights, "band", axis=0, tiled=True)

    def decode_tile(tile_index, block):
        tile_weights = lax.dynamic_index_in_dim(weights_all, tile_index, 0, keepdims=False)
        interp = jnp.dot(tile_weights, block, preferred_element_type=jnp.float32).astype(
            jnp.bfloat16
        )
        return decode_rows(
            interp, w_first[0], b_first[0], w_second[0], b_second[0], gain[0], w_out[0], b_out[0]
        )

    empty = jnp.zeros((channels, tile_count, cell_count), jnp.float32)
    my_index = lax.axis_index("patch")
    own_tiles = jnp.take(local_latents, block_rows.reshape(-1), axis=0).reshape(
        tile_count, -1, width
    )
    mine = (owners == my_index)[:, None, None]
    filled = jnp.where(mine, own_tiles.astype(jnp.float32), jnp.float32(0.0))
    all_blocks = lax.psum(filled.astype(jnp.bfloat16), "patch")

    def visit_summed(turn_index, buffer):
        tile_index = turn_index % tile_count
        block = lax.dynamic_index_in_dim(all_blocks, tile_index, 0, keepdims=False)
        result = decode_tile(tile_index, block)
        return lax.dynamic_update_index_in_dim(buffer, result, tile_index, 1)

    decoded = lax.fori_loop(0, tile_count, visit_summed, empty)
    regrid = lax.all_to_all(decoded, "patch", split_axis=1, concat_axis=2, tiled=True)
    return regrid.reshape(channels, -1)[None]


def solution(mesh):
    return jax.shard_map(
        body,
        mesh=mesh,
        in_specs=(
            P("band", "patch", None),
            P(),
            P(),
            P("band", "patch", None),
            P("band", None, None),
            P("band", None),
            P("band", None, None),
            P("band", None),
            P("band", None),
            P("band", None, None),
            P("band", None),
        ),
        out_specs=P("band", None, "patch"),
        check_vma=False,
    )
```

profile of v0, /device:TPU:0, one launch (start us, length us, event | category | flops | bytes accessed | tf_op | source)
XLA Modules:
  0.0 144.4 jit_solution(14935995324864705536)
XLA Ops:
  9.1 9.2 %gather_fusion = bf16[2048,512]{1,0:T(8,128)(2,1)} fusion(bf16[2560,512]{1,0:T(8,128)(2,1)S(1)} %bitcast.62, s32[2048]{0:T(1024)S(1)} %broadcast_clamp_fusion), kind=kCustom, calls=%fused_computation | custom fusion | bytes 4202496 | tf_op jit(solution)/shard_map/jit(_take)/gather | solution.py:53
  18.3 2.9 %select_convert_fusion = bf16[16,128,512]{2,1,0:T(8,128)(2,1)} fusion(bf16[16,128,512]{2,1,0:T(8,128)(2,1)} %bitcast.63, pred[16]{0:T(512)(128)(4,1)S(1)} %broadcast_compare_fusion, pred[16,128]{1,0:T(8,128)(4,1)S(1)} %compare_and_fusion), kind=kLoop, calls=%fused_computation.23 | loop fusion | flops 4194304 | bytes 4196368 | tf_op jit(solution)/shard_map/convert_element_type | solution.py:58
  21.9 53.7 %all-reduce.2.cloned.1.call-done = bf16[16,128,512]{2,1,0:T(8,128)(2,1)} async-done(((bf16[16,128,512]{2,1,0:T(8,128)(2,1)}), bf16[16,128,512]{2,1,0:T(8,128)(2,1)}) %all-reduce.2.cloned.1.call-update) | async-done | bytes 2097168 | tf_op jit(solution)/shard_map/psum | solution.py:58
  76.3 50.2 %while.15 = (s32[]{:T(128)}, f32[12,16,256]{2,0,1:T(8,128)}, bf16[16,256,128]{2,1,0:T(8,128)(2,1)}, bf16[16,128,512]{2,1,0:T(8,128)(2,1)}, bf16[1,512,512]{2,1,0...) while((s32[]{:T(128)}, f32[12,16,256]{2,0,1:T(8,128)}, ...), condition=%wide.region_4.5_spmd, body=%wide.region_1.4_spmd.sunk | while | flops 307236096 | bytes 3387677 | solution.py:66
  76.3 1.7 %multiply_convert_fusion.6 = bf16[256,512]{1,0:T(8,128)(2,1)S(1)} fusion(bf16[1,512,512]{2,1,0:T(8,128)(2,1)} %get-tuple-element.400, f32[512]{0:T(512)S(1)} %bitcast.71, bf16[16,128,512]{2,1,0:T(8,128)(2,1)} %get-tuple-element.399, s32[]{:T(128)S(6)} %select_n.74, bf16[16,256,128]{2,1,0:T(8,128)(2,1)} %get-tuple-element.398), kind=kOutput, calls=%fused_computation.11.clone.1 | convolution fusion | flops 168689664 | bytes 986112 | tf_op jit(solution)/shard_map/while/body/eval_jaxpr/dot_general | solution.py:9
  79.5 1.6 %multiply_convert_fusion.6 = bf16[256,512]{1,0:T(8,128)(2,1)S(1)} fusion(bf16[1,512,512]{2,1,0:T(8,128)(2,1)} %get-tuple-element.400, f32[512]{0:T(512)S(1)} %bitcast.71, bf16[16,128,512]{2,1,0:T(8,128)(2,1)} %get-tuple-element.399, s32[]{:T(128)S(6)} %select_n.74, bf16[16,256,128]{2,1,0:T(8,128)(2,1)} %get-tuple-element.398), kind=kOutput, calls=%fused_computation.11.clone.1 | convolution fusion | flops 168689664 | bytes 986112 | tf_op jit(solution)/shard_map/while/body/eval_jaxpr/dot_general | solution.py:9
  82.6 1.6 %multiply_convert_fusion.6 = bf16[256,512]{1,0:T(8,128)(2,1)S(1)} fusion(bf16[1,512,512]{2,1,0:T(8,128)(2,1)} %get-tuple-element.400, f32[512]{0:T(512)S(1)} %bitcast.71, bf16[16,128,512]{2,1,0:T(8,128)(2,1)} %get-tuple-element.399, s32[]{:T(128)S(6)} %select_n.74, bf16[16,256,128]{2,1,0:T(8,128)(2,1)} %get-tuple-element.398), kind=kOutput, calls=%fused_computation.11.clone.1 | convolution fusion | flops 168689664 | bytes 986112 | tf_op jit(solution)/shard_map/while/body/eval_jaxpr/dot_general | solution.py:9
  85.7 1.6 %multiply_convert_fusion.6 = bf16[256,512]{1,0:T(8,128)(2,1)S(1)} fusion(bf16[1,512,512]{2,1,0:T(8,128)(2,1)} %get-tuple-element.400, f32[512]{0:T(512)S(1)} %bitcast.71, bf16[16,128,512]{2,1,0:T(8,128)(2,1)} %get-tuple-element.399, s32[]{:T(128)S(6)} %select_n.74, bf16[16,256,128]{2,1,0:T(8,128)(2,1)} %get-tuple-element.398), kind=kOutput, calls=%fused_computation.11.clone.1 | convolution fusion | flops 168689664 | bytes 986112 | tf_op jit(solution)/shard_map/while/body/eval_jaxpr/dot_general | solution.py:9
  88.9 1.6 %multiply_convert_fusion.6 = bf16[256,512]{1,0:T(8,128)(2,1)S(1)} fusion(bf16[1,512,512]{2,1,0:T(8,128)(2,1)} %get-tuple-element.400, f32[512]{0:T(512)S(1)} %bitcast.71, bf16[16,128,512]{2,1,0:T(8,128)(2,1)} %get-tuple-element.399, s32[]{:T(128)S(6)} %select_n.74, bf16[16,256,128]{2,1,0:T(8,128)(2,1)} %get-tuple-element.398), kind=kOutput, calls=%fused_computation.11.clone.1 | convolution fusion | flops 168689664 | bytes 986112 | tf_op jit(solution)/shard_map/while/body/eval_jaxpr/dot_general | solution.py:9
  92.0 1.6 %multiply_convert_fusion.6 = bf16[256,512]{1,0:T(8,128)(2,1)S(1)} fusion(bf16[1,512,512]{2,1,0:T(8,128)(2,1)} %get-tuple-element.400, f32[512]{0:T(512)S(1)} %bitcast.71, bf16[16,128,512]{2,1,0:T(8,128)(2,1)} %get-tuple-element.399, s32[]{:T(128)S(6)} %select_n.74, bf16[16,256,128]{2,1,0:T(8,128)(2,1)} %get-tuple-element.398), kind=kOutput, calls=%fused_computation.11.clone.1 | convolution fusion | flops 168689664 | bytes 986112 | tf_op jit(solution)/shard_map/while/body/eval_jaxpr/dot_general | solution.py:9
  95.1 1.6 %multiply_convert_fusion.6 = bf16[256,512]{1,0:T(8,128)(2,1)S(1)} fusion(bf16[1,512,512]{2,1,0:T(8,128)(2,1)} %get-tuple-element.400, f32[512]{0:T(512)S(1)} %bitcast.71, bf16[16,128,512]{2,1,0:T(8,128)(2,1)} %get-tuple-element.399, s32[]{:T(128)S(6)} %select_n.74, bf16[16,256,128]{2,1,0:T(8,128)(2,1)} %get-tuple-element.398), kind=kOutput, calls=%fused_computation.11.clone.1 | convolution fusion | flops 168689664 | bytes 986112 | tf_op jit(solution)/shard_map/while/body/eval_jaxpr/dot_general | solution.py:9
  97.4 0.9 fusion.35
  98.3 1.6 %multiply_convert_fusion.6 = bf16[256,512]{1,0:T(8,128)(2,1)S(1)} fusion(bf16[1,512,512]{2,1,0:T(8,128)(2,1)} %get-tuple-element.400, f32[512]{0:T(512)S(1)} %bitcast.71, bf16[16,128,512]{2,1,0:T(8,128)(2,1)} %get-tuple-element.399, s32[]{:T(128)S(6)} %select_n.74, bf16[16,256,128]{2,1,0:T(8,128)(2,1)} %get-tuple-element.398), kind=kOutput, calls=%fused_computation.11.clone.1 | convolution fusion | flops 168689664 | bytes 986112 | tf_op jit(solution)/shard_map/while/body/eval_jaxpr/dot_general | solution.py:9
  101.4 1.6 %multiply_convert_fusion.6 = bf16[256,512]{1,0:T(8,128)(2,1)S(1)} fusion(bf16[1,512,512]{2,1,0:T(8,128)(2,1)} %get-tuple-element.400, f32[512]{0:T(512)S(1)} %bitcast.71, bf16[16,128,512]{2,1,0:T(8,128)(2,1)} %get-tuple-element.399, s32[]{:T(128)S(6)} %select_n.74, bf16[16,256,128]{2,1,0:T(8,128)(2,1)} %get-tuple-element.398), kind=kOutput, calls=%fused_computation.11.clone.1 | convolution fusion | flops 168689664 | bytes 986112 | tf_op jit(solution)/shard_map/while/body/eval_jaxpr/dot_general | solution.py:9
  104.6 1.6 %multiply_convert_fusion.6 = bf16[256,512]{1,0:T(8,128)(2,1)S(1)} fusion(bf16[1,512,512]{2,1,0:T(8,128)(2,1)} %get-tuple-element.400, f32[512]{0:T(512)S(1)} %bitcast.71, bf16[16,128,512]{2,1,0:T(8,128)(2,1)} %get-tuple-element.399, s32[]{:T(128)S(6)} %select_n.74, bf16[16,256,128]{2,1,0:T(8,128)(2,1)} %get-tuple-element.398), kind=kOutput, calls=%fused_computation.11.clone.1 | convolution fusion | flops 168689664 | bytes 986112 | tf_op jit(solution)/shard_map/while/body/eval_jaxpr/dot_general | solution.py:9
  107.7 1.6 %multiply_convert_fusion.6 = bf16[256,512]{1,0:T(8,128)(2,1)S(1)} fusion(bf16[1,512,512]{2,1,0:T(8,128)(2,1)} %get-tuple-element.400, f32[512]{0:T(512)S(1)} %bitcast.71, bf16[16,128,512]{2,1,0:T(8,128)(2,1)} %get-tuple-element.399, s32[]{:T(128)S(6)} %select_n.74, bf16[16,256,128]{2,1,0:T(8,128)(2,1)} %get-tuple-element.398), kind=kOutput, calls=%fused_computation.11.clone.1 | convolution fusion | flops 168689664 | bytes 986112 | tf_op jit(solution)/shard_map/while/body/eval_jaxpr/dot_general | solution.py:9
  110.8 1.6 %multiply_convert_fusion.6 = bf16[256,512]{1,0:T(8,128)(2,1)S(1)} fusion(bf16[1,512,512]{2,1,0:T(8,128)(2,1)} %get-tuple-element.400, f32[512]{0:T(512)S(1)} %bitcast.71, bf16[16,128,512]{2,1,0:T(8,128)(2,1)} %get-tuple-element.399, s32[]{:T(128)S(6)} %select_n.74, bf16[16,256,128]{2,1,0:T(8,128)(2,1)} %get-tuple-element.398), kind=kOutput, calls=%fused_computation.11.clone.1 | convolution fusion | flops 168689664 | bytes 986112 | tf_op jit(solution)/shard_map/while/body/eval_jaxpr/dot_general | solution.py:9
  113.1 0.9 fusion.35
  114.0 1.7 %multiply_convert_fusion.6 = bf16[256,512]{1,0:T(8,128)(2,1)S(1)} fusion(bf16[1,512,512]{2,1,0:T(8,128)(2,1)} %get-tuple-element.400, f32[512]{0:T(512)S(1)} %bitcast.71, bf16[16,128,512]{2,1,0:T(8,128)(2,1)} %get-tuple-element.399, s32[]{:T(128)S(6)} %select_n.74, bf16[16,256,128]{2,1,0:T(8,128)(2,1)} %get-tuple-element.398), kind=kOutput, calls=%fused_computation.11.clone.1 | convolution fusion | flops 168689664 | bytes 986112 | tf_op jit(solution)/shard_map/while/body/eval_jaxpr/dot_general | solution.py:9
  117.1 1.6 %multiply_convert_fusion.6 = bf16[256,512]{1,0:T(8,128)(2,1)S(1)} fusion(bf16[1,512,512]{2,1,0:T(8,128)(2,1)} %get-tuple-element.400, f32[512]{0:T(512)S(1)} %bitcast.71, bf16[16,128,512]{2,1,0:T(8,128)(2,1)} %get-tuple-element.399, s32[]{:T(128)S(6)} %select_n.74, bf16[16,256,128]{2,1,0:T(8,128)(2,1)} %get-tuple-element.398), kind=kOutput, calls=%fused_computation.11.clone.1 | convolution fusion | flops 168689664 | bytes 986112 | tf_op jit(solution)/shard_map/while/body/eval_jaxpr/dot_general | solution.py:9
  120.2 1.6 %multiply_convert_fusion.6 = bf16[256,512]{1,0:T(8,128)(2,1)S(1)} fusion(bf16[1,512,512]{2,1,0:T(8,128)(2,1)} %get-tuple-element.400, f32[512]{0:T(512)S(1)} %bitcast.71, bf16[16,128,512]{2,1,0:T(8,128)(2,1)} %get-tuple-element.399, s32[]{:T(128)S(6)} %select_n.74, bf16[16,256,128]{2,1,0:T(8,128)(2,1)} %get-tuple-element.398), kind=kOutput, calls=%fused_computation.11.clone.1 | convolution fusion | flops 168689664 | bytes 986112 | tf_op jit(solution)/shard_map/while/body/eval_jaxpr/dot_general | solution.py:9
  123.4 1.6 %multiply_convert_fusion.6 = bf16[256,512]{1,0:T(8,128)(2,1)S(1)} fusion(bf16[1,512,512]{2,1,0:T(8,128)(2,1)} %get-tuple-element.400, f32[512]{0:T(512)S(1)} %bitcast.71, bf16[16,128,512]{2,1,0:T(8,128)(2,1)} %get-tuple-element.399, s32[]{:T(128)S(6)} %select_n.74, bf16[16,256,128]{2,1,0:T(8,128)(2,1)} %get-tuple-element.398), kind=kOutput, calls=%fused_computation.11.clone.1 | convolution fusion | flops 168689664 | bytes 986112 | tf_op jit(solution)/shard_map/while/body/eval_jaxpr/dot_general | solution.py:9
  126.5 9.4 %all_to_all.15 = f32[12,16,256]{2,0,1:T(8,128)S(1)} all-to-all(f32[12,16,256]{2,0,1:T(8,128)} %get-tuple-element.270), channel_id=1, replica_groups=mesh['band'=8,'patch'=4] {'patch'}, dimensions={1} | all-to-all | bytes 393216 | tf_op jit(solution)/shard_map/all_to_all | solution.py:67
  136.0 0.9 broadcast_in_dim_reshape.3
  (105 shorter events, 25.0 us)
Async XLA Ops:
  7.4 1.8 %copy-start = (bf16[1,2560,512]{2,1,0:T(8,128)(2,1)S(1)}, bf16[1,2560,512]{2,1,0:T(8,128)(2,1)}, u32[]{:S(2)}) copy-start(bf16[1,2560,512]{2,1,0:T(8,128)(2,1)} %param.13) | copy-start | bytes 7864324
  7.4 68.2 %all-reduce.2.cloned.1.call-start = ((), (), s32[]{:S(2)}) async-start(), calls=%async_computation.2 | async-start | bytes 4194304 | tf_op jit(solution)/shard_map/psum | solution.py:58
  9.1 9.2 %copy-start.7 = (s32[16]{0:T(128)S(1)}, s32[16]{0:T(128)}, u32[]{:S(2)}) copy-start(s32[16]{0:T(128)} %param.14) | copy-start | bytes 196
  21.2 55.1 %copy-start.1 = (bf16[1,512,512]{2,1,0:T(8,128)(2,1)S(1)}, bf16[1,512,512]{2,1,0:T(8,128)(2,1)}, u32[]{:S(2)}) copy-start(bf16[1,512,512]{2,1,0:T(8,128)(2,1)} %param.19) | copy-start | bytes 1572868
  21.2 55.1 %copy-start.2 = (bf16[1,12,512]{2,1,0:T(8,128)(2,1)S(1)}, bf16[1,12,512]{2,1,0:T(8,128)(2,1)}, u32[]{:S(2)}) copy-start(bf16[1,12,512]{2,1,0:T(8,128)(2,1)} %param.22) | copy-start | bytes 36868
  21.2 55.1 %copy-start.3 = (f32[1,512]{1,0:T(1,128)S(1)}, f32[1,512]{1,0:T(1,128)}, u32[]{:S(2)}) copy-start(f32[1,512]{1,0:T(1,128)} %param.20) | copy-start | bytes 6148
  21.2 55.1 %copy-start.4 = (f32[1,512]{1,0:T(1,128)S(1)}, f32[1,512]{1,0:T(1,128)}, u32[]{:S(2)}) copy-start(f32[1,512]{1,0:T(1,128)} %param.21) | copy-start | bytes 6148
  21.2 55.1 %copy-start.5 = (f32[1,12]{1,0:T(1,128)S(1)}, f32[1,12]{1,0:T(1,128)}, u32[]{:S(2)}) copy-start(f32[1,12]{1,0:T(1,128)} %param.23) | copy-start | bytes 148
  21.2 55.1 %copy-start.6 = (f32[1,512]{1,0:T(1,128)S(1)}, f32[1,512]{1,0:T(1,128)}, u32[]{:S(2)}) copy-start(f32[1,512]{1,0:T(1,128)} %param.18) | copy-start | bytes 6148
  21.3 54.3 %all-gather.2.cloned.1.call-start = ((), (), s32[]{:S(2)}) async-start(), calls=%async_computation.1 | async-start | bytes 1179648 | tf_op jit(solution)/shard_map/all_gather | solution.py:40
Sparse Core Ops, SparseCore 0:
  21.4 54.1 all-reduce.1
Sparse Core Ops, SparseCore 1:
  23.9 43.0 all-gather.1
where the time goes:
time: 145 us; the launch traced here: 144 us
  waiting for transfers between devices  54.2 us (37%)
  matrix products  46.4 us (32%)
  between operations  14.9 us (10%)
  local copies, waits for them, and re-layouts  11.2 us (8%)
  blocking collectives  9.38 us (6%)
  other arithmetic  7.95 us (5%)
    psum x1, waiting for transfers between devices, body(): all_blocks = lax.psum(filled.astype(jnp.bfloat16), 'patch')  53.7 us
    dot_general x16, matrix products, decode_rows(): jnp.dot(interp, w_first, preferred_element_type=jnp.float32) + b_first  26.3 us
    dot_general x16, matrix products, decode_rows(): lax.dot_general(w_out, normed, (((1,), (1,)), ((), ())), preferred_elemen...  13.9 us
    all_to_all x1, blocking collectives, body(): lax.all_to_all(decoded, 'patch', split_axis=1, concat_axis=2, tiled=True)  9.38 us
    gather x1, local copies, waits for them, and re-layouts, body(): jnp.take(local_latents, block_rows.reshape(-1), axis=0)  9.18 us
    dot_general x16, matrix products, decode_rows(): jnp.dot(hidden, w_second, preferred_element_type=jnp.float32) + b_second  6.16 us
    reduce_sum x16, other arithmetic, decode_rows(): variance = jnp.mean(centred * centred, axis=-1, keepdims=True)  3.28 us
    convert_element_type x1, other arithmetic, body(): all_blocks = lax.psum(filled.astype(jnp.bfloat16), 'patch')  2.9 us
  transfers between devices with their start and end apart: 2, of which 1 were waited for; matrix products, arithmetic and copies ran while one was open for 0% of the time, Pallas kernels for 0%

commit v1 on v0

--- a/solution.py
+++ b/solution.py
@@ -64,7 +64,10 @@
         return lax.dynamic_update_index_in_dim(buffer, result, tile_index, 1)
 
     decoded = lax.fori_loop(0, tile_count, visit_summed, empty)
-    regrid = lax.all_to_all(decoded, "patch", split_axis=1, concat_axis=2, tiled=True)
+    devices = lax.axis_size("patch")
+    tiles = jnp.stack(jnp.split(decoded, devices, axis=1), axis=0)
+    tiles = lax.all_to_all(tiles, "patch", split_axis=0, concat_axis=0)
+    regrid = jnp.concatenate(tiles, axis=2)
     return regrid.reshape(channels, -1)[None]
 
 

time: 145 us -> 161 us (1.11)
  local copies, waits for them, and re-layouts: 11.2 us -> 37.9 us
  matrix products: 46.4 us -> 36.7 us
  blocking collectives: 9.38 us -> 7.67 us
    dynamic_update_slice x0 -> x32, local copies, waits for them, and re-layouts: none -> 25.6 us  [visit_summed(): return lax.dynamic_update_index_in_dim(buffer, result, tile_index, 1)]
    dot_general x16, matrix products: 13.9 us -> 4.14 us  [decode_rows(): lax.dot_general(w_out, normed, (((1,), (1,)), ((), ())), preferred_elemen...]
    all_to_all x1, blocking collectives: 9.38 us -> 7.67 us  [body(): tiles = lax.all_to_all(tiles, 'patch', split_axis=0, concat_axis=0)]
where the time goes in v1:
time: 161 us; the launch traced here: 160 us
  waiting for transfers between devices  54.2 us (34%)
  local copies, waits for them, and re-layouts  37.9 us (24%)
  matrix products  36.7 us (23%)
  between operations  14.9 us (9%)
  other arithmetic  7.99 us (5%)
  blocking collectives  7.67 us (5%)
    psum x1, waiting for transfers between devices, body(): all_blocks = lax.psum(filled.astype(jnp.bfloat16), 'patch')  53.7 us
    dot_general x16, matrix products, decode_rows(): jnp.dot(interp, w_first, preferred_element_type=jnp.float32) + b_first  26.4 us
    dynamic_update_slice x32, local copies, waits for them, and re-layouts, visit_summed(): return lax.dynamic_update_index_in_dim(buffer, result, tile_index, 1)  25.6 us
    gather x1, local copies, waits for them, and re-layouts, body(): jnp.take(local_latents, block_rows.reshape(-1), axis=0)  9.21 us
    all_to_all x1, blocking collectives, body(): tiles = lax.all_to_all(tiles, 'patch', split_axis=0, concat_axis=0)  7.67 us
    dot_general x16, matrix products, decode_rows(): jnp.dot(hidden, w_second, preferred_element_type=jnp.float32) + b_second  6.16 us
    dot_general x16, matrix products, decode_rows(): lax.dot_general(w_out, normed, (((1,), (1,)), ((), ())), preferred_elemen...  4.14 us
    reduce_sum x16, other arithmetic, decode_rows(): variance = jnp.mean(centred * centred, axis=-1, keepdims=True)  3.28 us
  transfers between devices with their start and end apart: 2, of which 1 were waited for; matrix products, arithmetic and copies ran while one was open for 0% of the time, Pallas kernels for 0%

profile of v1, /device:TPU:0, one launch (start us, length us, event | category | flops | bytes accessed | tf_op | source)
XLA Modules:
  0.0 159.9 jit_solution(8485834692615193543)
XLA Ops:
  9.1 9.2 %gather_fusion = bf16[2048,512]{1,0:T(8,128)(2,1)} fusion(bf16[2560,512]{1,0:T(8,128)(2,1)S(1)} %bitcast.65, s32[2048]{0:T(1024)S(1)} %broadcast_clamp_fusion), kind=kCustom, calls=%fused_computation | custom fusion | bytes 4202496 | tf_op jit(solution)/shard_map/jit(_take)/gather | solution.py:53
  18.3 2.9 %select_convert_fusion = bf16[16,128,512]{2,1,0:T(8,128)(2,1)} fusion(bf16[16,128,512]{2,1,0:T(8,128)(2,1)} %bitcast.66, pred[16]{0:T(512)(128)(4,1)S(1)} %broadcast_compare_fusion, pred[16,128]{1,0:T(8,128)(4,1)S(1)} %compare_and_fusion), kind=kLoop, calls=%fused_computation.22 | loop fusion | flops 4194304 | bytes 4196368 | tf_op jit(solution)/shard_map/convert_element_type | solution.py:58
  21.9 53.7 %all-reduce.2.cloned.1.call-done = bf16[16,128,512]{2,1,0:T(8,128)(2,1)} async-done(((bf16[16,128,512]{2,1,0:T(8,128)(2,1)}), bf16[16,128,512]{2,1,0:T(8,128)(2,1)}) %all-reduce.2.cloned.1.call-update) | async-done | bytes 2097168 | tf_op jit(solution)/shard_map/psum | solution.py:58
  76.3 66.3 %while.15 = (s32[]{:T(128)}, f32[12,16,256]{2,1,0:T(8,128)}, bf16[16,256,128]{2,1,0:T(8,128)(2,1)}, bf16[16,128,512]{2,1,0:T(8,128)(2,1)}, bf16[1,512,512]{2,1,0...) while((s32[]{:T(128)}, f32[12,16,256]{2,1,0:T(8,128)}, ...), condition=%wide.region_4.5_spmd, body=%wide.region_1.4_spmd.sunk | while | flops 307236096 | bytes 3432733 | solution.py:66
  76.3 1.7 %multiply_convert_fusion.6 = bf16[256,512]{1,0:T(8,128)(2,1)S(1)} fusion(bf16[1,512,512]{2,1,0:T(8,128)(2,1)} %get-tuple-element.404, f32[512]{0:T(512)S(1)} %bitcast.73, bf16[16,128,512]{2,1,0:T(8,128)(2,1)} %get-tuple-element.403, s32[]{:T(128)S(6)} %select_n.74, bf16[16,256,128]{2,1,0:T(8,128)(2,1)} %get-tuple-element.402), kind=kOutput, calls=%fused_computation.10.clone.1 | convolution fusion | flops 168689664 | bytes 986112 | tf_op jit(solution)/shard_map/while/body/eval_jaxpr/dot_general | solution.py:9
  80.5 1.6 %multiply_convert_fusion.6 = bf16[256,512]{1,0:T(8,128)(2,1)S(1)} fusion(bf16[1,512,512]{2,1,0:T(8,128)(2,1)} %get-tuple-element.404, f32[512]{0:T(512)S(1)} %bitcast.73, bf16[16,128,512]{2,1,0:T(8,128)(2,1)} %get-tuple-element.403, s32[]{:T(128)S(6)} %select_n.74, bf16[16,256,128]{2,1,0:T(8,128)(2,1)} %get-tuple-element.402), kind=kOutput, calls=%fused_computation.10.clone.1 | convolution fusion | flops 168689664 | bytes 986112 | tf_op jit(solution)/shard_map/while/body/eval_jaxpr/dot_general | solution.py:9
  83.0 1.6 dynamic_update_slice.12
  84.6 1.6 %multiply_convert_fusion.6 = bf16[256,512]{1,0:T(8,128)(2,1)S(1)} fusion(bf16[1,512,512]{2,1,0:T(8,128)(2,1)} %get-tuple-element.404, f32[512]{0:T(512)S(1)} %bitcast.73, bf16[16,128,512]{2,1,0:T(8,128)(2,1)} %get-tuple-element.403, s32[]{:T(128)S(6)} %select_n.74, bf16[16,256,128]{2,1,0:T(8,128)(2,1)} %get-tuple-element.402), kind=kOutput, calls=%fused_computation.10.clone.1 | convolution fusion | flops 168689664 | bytes 986112 | tf_op jit(solution)/shard_map/while/body/eval_jaxpr/dot_general | solution.py:9
  87.2 1.6 dynamic_update_slice.12
  88.7 1.7 %multiply_convert_fusion.6 = bf16[256,512]{1,0:T(8,128)(2,1)S(1)} fusion(bf16[1,512,512]{2,1,0:T(8,128)(2,1)} %get-tuple-element.404, f32[512]{0:T(512)S(1)} %bitcast.73, bf16[16,128,512]{2,1,0:T(8,128)(2,1)} %get-tuple-element.403, s32[]{:T(128)S(6)} %select_n.74, bf16[16,256,128]{2,1,0:T(8,128)(2,1)} %get-tuple-element.402), kind=kOutput, calls=%fused_computation.10.clone.1 | convolution fusion | flops 168689664 | bytes 986112 | tf_op jit(solution)/shard_map/while/body/eval_jaxpr/dot_general | solution.py:9
  91.3 1.6 dynamic_update_slice.12
  92.9 1.7 %multiply_convert_fusion.6 = bf16[256,512]{1,0:T(8,128)(2,1)S(1)} fusion(bf16[1,512,512]{2,1,0:T(8,128)(2,1)} %get-tuple-element.404, f32[512]{0:T(512)S(1)} %bitcast.73, bf16[16,128,512]{2,1,0:T(8,128)(2,1)} %get-tuple-element.403, s32[]{:T(128)S(6)} %select_n.74, bf16[16,256,128]{2,1,0:T(8,128)(2,1)} %get-tuple-element.402), kind=kOutput, calls=%fused_computation.10.clone.1 | convolution fusion | flops 168689664 | bytes 986112 | tf_op jit(solution)/shard_map/while/body/eval_jaxpr/dot_general | solution.py:9
  97.0 1.7 %multiply_convert_fusion.6 = bf16[256,512]{1,0:T(8,128)(2,1)S(1)} fusion(bf16[1,512,512]{2,1,0:T(8,128)(2,1)} %get-tuple-element.404, f32[512]{0:T(512)S(1)} %bitcast.73, bf16[16,128,512]{2,1,0:T(8,128)(2,1)} %get-tuple-element.403, s32[]{:T(128)S(6)} %select_n.74, bf16[16,256,128]{2,1,0:T(8,128)(2,1)} %get-tuple-element.402), kind=kOutput, calls=%fused_computation.10.clone.1 | convolution fusion | flops 168689664 | bytes 986112 | tf_op jit(solution)/shard_map/while/body/eval_jaxpr/dot_general | solution.py:9
  101.2 1.7 %multiply_convert_fusion.6 = bf16[256,512]{1,0:T(8,128)(2,1)S(1)} fusion(bf16[1,512,512]{2,1,0:T(8,128)(2,1)} %get-tuple-element.404, f32[512]{0:T(512)S(1)} %bitcast.73, bf16[16,128,512]{2,1,0:T(8,128)(2,1)} %get-tuple-element.403, s32[]{:T(128)S(6)} %select_n.74, bf16[16,256,128]{2,1,0:T(8,128)(2,1)} %get-tuple-element.402), kind=kOutput, calls=%fused_computation.10.clone.1 | convolution fusion | flops 168689664 | bytes 986112 | tf_op jit(solution)/shard_map/while/body/eval_jaxpr/dot_general | solution.py:9
  105.3 1.7 %multiply_convert_fusion.6 = bf16[256,512]{1,0:T(8,128)(2,1)S(1)} fusion(bf16[1,512,512]{2,1,0:T(8,128)(2,1)} %get-tuple-element.404, f32[512]{0:T(512)S(1)} %bitcast.73, bf16[16,128,512]{2,1,0:T(8,128)(2,1)} %get-tuple-element.403, s32[]{:T(128)S(6)} %select_n.74, bf16[16,256,128]{2,1,0:T(8,128)(2,1)} %get-tuple-element.402), kind=kOutput, calls=%fused_computation.10.clone.1 | convolution fusion | flops 168689664 | bytes 986112 | tf_op jit(solution)/shard_map/while/body/eval_jaxpr/dot_general | solution.py:9
  109.5 1.7 %multiply_convert_fusion.6 = bf16[256,512]{1,0:T(8,128)(2,1)S(1)} fusion(bf16[1,512,512]{2,1,0:T(8,128)(2,1)} %get-tuple-element.404, f32[512]{0:T(512)S(1)} %bitcast.73, bf16[16,128,512]{2,1,0:T(8,128)(2,1)} %get-tuple-element.403, s32[]{:T(128)S(6)} %select_n.74, bf16[16,256,128]{2,1,0:T(8,128)(2,1)} %get-tuple-element.402), kind=kOutput, calls=%fused_computation.10.clone.1 | convolution fusion | flops 168689664 | bytes 986112 | tf_op jit(solution)/shard_map/while/body/eval_jaxpr/dot_general | solution.py:9
  113.6 1.6 %multiply_convert_fusion.6 = bf16[256,512]{1,0:T(8,128)(2,1)S(1)} fusion(bf16[1,512,512]{2,1,0:T(8,128)(2,1)} %get-tuple-element.404, f32[512]{0:T(512)S(1)} %bitcast.73, bf16[16,128,512]{2,1,0:T(8,128)(2,1)} %get-tuple-element.403, s32[]{:T(128)S(6)} %select_n.74, bf16[16,256,128]{2,1,0:T(8,128)(2,1)} %get-tuple-element.402), kind=kOutput, calls=%fused_computation.10.clone.1 | convolution fusion | flops 168689664 | bytes 986112 | tf_op jit(solution)/shard_map/while/body/eval_jaxpr/dot_general | solution.py:9
  117.7 1.6 %multiply_convert_fusion.6 = bf16[256,512]{1,0:T(8,128)(2,1)S(1)} fusion(bf16[1,512,512]{2,1,0:T(8,128)(2,1)} %get-tuple-element.404, f32[512]{0:T(512)S(1)} %bitcast.73, bf16[16,128,512]{2,1,0:T(8,128)(2,1)} %get-tuple-element.403, s32[]{:T(128)S(6)} %select_n.74, bf16[16,256,128]{2,1,0:T(8,128)(2,1)} %get-tuple-element.402), kind=kOutput, calls=%fused_computation.10.clone.1 | convolution fusion | flops 168689664 | bytes 986112 | tf_op jit(solution)/shard_map/while/body/eval_jaxpr/dot_general | solution.py:9
  121.9 1.6 %multiply_convert_fusion.6 = bf16[256,512]{1,0:T(8,128)(2,1)S(1)} fusion(bf16[1,512,512]{2,1,0:T(8,128)(2,1)} %get-tuple-element.404, f32[512]{0:T(512)S(1)} %bitcast.73, bf16[16,128,512]{2,1,0:T(8,128)(2,1)} %get-tuple-element.403, s32[]{:T(128)S(6)} %select_n.74, bf16[16,256,128]{2,1,0:T(8,128)(2,1)} %get-tuple-element.402), kind=kOutput, calls=%fused_computation.10.clone.1 | convolution fusion | flops 168689664 | bytes 986112 | tf_op jit(solution)/shard_map/while/body/eval_jaxpr/dot_general | solution.py:9
  126.0 1.6 %multiply_convert_fusion.6 = bf16[256,512]{1,0:T(8,128)(2,1)S(1)} fusion(bf16[1,512,512]{2,1,0:T(8,128)(2,1)} %get-tuple-element.404, f32[512]{0:T(512)S(1)} %bitcast.73, bf16[16,128,512]{2,1,0:T(8,128)(2,1)} %get-tuple-element.403, s32[]{:T(128)S(6)} %select_n.74, bf16[16,256,128]{2,1,0:T(8,128)(2,1)} %get-tuple-element.402), kind=kOutput, calls=%fused_computation.10.clone.1 | convolution fusion | flops 168689664 | bytes 986112 | tf_op jit(solution)/shard_map/while/body/eval_jaxpr/dot_general | solution.py:9
  130.1 1.6 %multiply_convert_fusion.6 = bf16[256,512]{1,0:T(8,128)(2,1)S(1)} fusion(bf16[1,512,512]{2,1,0:T(8,128)(2,1)} %get-tuple-element.404, f32[512]{0:T(512)S(1)} %bitcast.73, bf16[16,128,512]{2,1,0:T(8,128)(2,1)} %get-tuple-element.403, s32[]{:T(128)S(6)} %select_n.74, bf16[16,256,128]{2,1,0:T(8,128)(2,1)} %get-tuple-element.402), kind=kOutput, calls=%fused_computation.10.clone.1 | convolution fusion | flops 168689664 | bytes 986112 | tf_op jit(solution)/shard_map/while/body/eval_jaxpr/dot_general | solution.py:9
  134.3 1.7 %multiply_convert_fusion.6 = bf16[256,512]{1,0:T(8,128)(2,1)S(1)} fusion(bf16[1,512,512]{2,1,0:T(8,128)(2,1)} %get-tuple-element.404, f32[512]{0:T(512)S(1)} %bitcast.73, bf16[16,128,512]{2,1,0:T(8,128)(2,1)} %get-tuple-element.403, s32[]{:T(128)S(6)} %select_n.74, bf16[16,256,128]{2,1,0:T(8,128)(2,1)} %get-tuple-element.402), kind=kOutput, calls=%fused_computation.10.clone.1 | convolution fusion | flops 168689664 | bytes 986112 | tf_op jit(solution)/shard_map/while/body/eval_jaxpr/dot_general | solution.py:9
  138.4 1.7 %multiply_convert_fusion.6 = bf16[256,512]{1,0:T(8,128)(2,1)S(1)} fusion(bf16[1,512,512]{2,1,0:T(8,128)(2,1)} %get-tuple-element.404, f32[512]{0:T(512)S(1)} %bitcast.73, bf16[16,128,512]{2,1,0:T(8,128)(2,1)} %get-tuple-element.403, s32[]{:T(128)S(6)} %select_n.74, bf16[16,256,128]{2,1,0:T(8,128)(2,1)} %get-tuple-element.402), kind=kOutput, calls=%fused_computation.10.clone.1 | convolution fusion | flops 168689664 | bytes 986112 | tf_op jit(solution)/shard_map/while/body/eval_jaxpr/dot_general | solution.py:9
  143.7 7.7 %all_to_all.5 = f32[4,12,4,256]{3,2,1,0:T(4,128)S(1)} all-to-all(f32[4,12,4,256]{3,2,1,0:T(4,128)S(1)} %pad_maximum_fusion), channel_id=1, replica_groups=mesh['band'=8,'patch'=4] {'patch'}, dimensions={0} | all-to-all | bytes 393216 | tf_op jit(solution)/shard_map/all_to_all | solution.py:69
  (139 shorter events, 39.9 us)
Async XLA Ops:
  7.4 1.8 %copy-start = (bf16[1,2560,512]{2,1,0:T(8,128)(2,1)S(1)}, bf16[1,2560,512]{2,1,0:T(8,128)(2,1)}, u32[]{:S(2)}) copy-start(bf16[1,2560,512]{2,1,0:T(8,128)(2,1)} %param.13) | copy-start | bytes 7864324
  7.4 68.2 %all-reduce.2.cloned.1.call-start = ((), (), s32[]{:S(2)}) async-start(), calls=%async_computation.2 | async-start | bytes 4194304 | tf_op jit(solution)/shard_map/psum | solution.py:58
  9.1 9.2 %copy-start.7 = (s32[16]{0:T(128)S(1)}, s32[16]{0:T(128)}, u32[]{:S(2)}) copy-start(s32[16]{0:T(128)} %param.14) | copy-start | bytes 196
  21.2 55.0 %copy-start.1 = (bf16[1,512,512]{2,1,0:T(8,128)(2,1)S(1)}, bf16[1,512,512]{2,1,0:T(8,128)(2,1)}, u32[]{:S(2)}) copy-start(bf16[1,512,512]{2,1,0:T(8,128)(2,1)} %param.19) | copy-start | bytes 1572868
  21.2 55.0 %copy-start.2 = (bf16[1,12,512]{2,1,0:T(8,128)(2,1)S(1)}, bf16[1,12,512]{2,1,0:T(8,128)(2,1)}, u32[]{:S(2)}) copy-start(bf16[1,12,512]{2,1,0:T(8,128)(2,1)} %param.22) | copy-start | bytes 36868
  21.2 55.0 %copy-start.3 = (f32[1,512]{1,0:T(1,128)S(1)}, f32[1,512]{1,0:T(1,128)}, u32[]{:S(2)}) copy-start(f32[1,512]{1,0:T(1,128)} %param.20) | copy-start | bytes 6148
  21.3 55.0 %copy-start.4 = (f32[1,512]{1,0:T(1,128)S(1)}, f32[1,512]{1,0:T(1,128)}, u32[]{:S(2)}) copy-start(f32[1,512]{1,0:T(1,128)} %param.21) | copy-start | bytes 6148
  21.3 55.0 %copy-start.5 = (f32[1,12]{1,0:T(1,128)S(1)}, f32[1,12]{1,0:T(1,128)}, u32[]{:S(2)}) copy-start(f32[1,12]{1,0:T(1,128)} %param.23) | copy-start | bytes 148
  21.3 55.0 %copy-start.6 = (f32[1,512]{1,0:T(1,128)S(1)}, f32[1,512]{1,0:T(1,128)}, u32[]{:S(2)}) copy-start(f32[1,512]{1,0:T(1,128)} %param.18) | copy-start | bytes 6148
  21.3 54.3 %all-gather.2.cloned.1.call-start = ((), (), s32[]{:S(2)}) async-start(), calls=%async_computation.1 | async-start | bytes 1179648 | tf_op jit(solution)/shard_map/all_gather | solution.py:40
Sparse Core Ops, SparseCore 0:
  21.4 54.1 all-reduce.1
Sparse Core Ops, SparseCore 1:
  23.9 43.0 all-gather.1
